TPU v7x, 32 devices: a whole 2x2x4 slice. The times are simulated.
32 devices in a mesh: layer: 2 (over core), row: 4 (over y, x), col: 4 (over z).
Axes of the slice: x: 2, y: 2, z: 4, core: 2. Of those that a mesh axis runs over, the one named last changes fastest.
Arguments:
- left_matrix: bfloat16 [2048, 16384], P('row', ('layer', 'col')), may hold values from -6 to 6
- right_matrix: bfloat16 [16384, 8192], P(('layer', 'row'), 'col'), may hold values from -0.046875 to 0.046875
Outputs:
- product: bfloat16 [2048, 8192], P(('row', 'layer'), 'col')
All inputs are finite; a program needn't handle non-finite values.
Results may differ from a plain program's by a relative error of at most 0.001.
Values may be sent and summed in bfloat16 or wider, within the bound.
A program may use at most 128 MiB of HBM per device.

v0:
```python
import jax
import jax.numpy as jnp
from jax import lax
from jax.sharding import PartitionSpec as P


def local(left_matrix, right_matrix):
    left_rows = lax.all_gather(left_matrix, "col", axis=1, tiled=True)
    right_joined = lax.all_gather(right_matrix, "row", axis=0, tiled=True)
    summed = lax.psum_scatter(
        jnp.dot(left_rows, right_joined, preferred_element_type=jnp.float32),
        "layer",
        scatter_dimension=0,
        tiled=True,
    )
    return summed.astype(jnp.bfloat16)


def solution(mesh):
    in_specs = (P("row", ("layer", "col")), P(("layer", "row"), "col"))
    out_specs = P(("row", "layer"), "col")
    return jax.shard_map(local, mesh=mesh, in_specs=in_specs, out_specs=out_specs, check_vma=False)
```

profile of v0, /device:TPU:5, one launch (start us, length us, event | category | flops | bytes accessed | tf_op | source)
XLA Modules:
  0.0 503.8 jit_solution(16767280769241972368)
XLA Ops:
  6.5 0.0 all-gather.3.cloned.1.call-start
  6.5 0.7 all-gather.3.cloned.1.call-update
  7.3 0.0 all-gather.5.cloned.1.call-start
  7.3 0.7 all-gather.5.cloned.1.call-update
  8.0 0.0 reduce-scatter.2.cloned.1.call-start
  8.1 151.9 %all-gather.3.cloned.1.call-done = bf16[512,8192]{1,0:T(8,128)(2,1)} async-done(((bf16[512,2048]{1,0:T(8,128)(2,1)}), bf16[512,8192]{1,0:T(8,128)(2,1)}) %all-gather.3.cloned.1.call-update) | async-done | bytes 8388624 | tf_op jit(solution)/shard_map/all_gather | solution.py:8
  159.9 296.8 %all-gather.5.cloned.1.call-done = bf16[8192,2048]{1,0:T(8,128)(2,1)} async-done(((bf16[2048,2048]{1,0:T(8,128)(2,1)}), bf16[8192,2048]{1,0:T(8,128)(2,1)}) %all-gather.5.cloned.1.call-update) | async-done | bytes 33554448 | tf_op jit(solution)/shard_map/all_gather | solution.py:9
  456.7 24.8 %fusion = f32[512,2048]{1,0:T(8,128)} fusion(bf16[512,8192]{1,0:T(8,128)(2,1)} %all-gather.3.cloned.1.call-done, bf16[8192,2048]{1,0:T(8,128)(2,1)} %all-gather.5.cloned.1.call-done), kind=kOutput, calls=%fused_computation | convolution fusion | flops 17179869184 | bytes 46137344 | tf_op jit(solution)/shard_map/dot_general | solution.py:11
  481.5 0.0 reduce-scatter.2.cloned.1.call-update
  481.5 13.1 %reduce-scatter.2.cloned.1.call-done = f32[256,2048]{1,0:T(8,128)} async-done(((f32[512,2048]{1,0:T(8,128)}), f32[256,2048]{1,0:T(8,128)}) %reduce-scatter.2.cloned.1.call-update) | async-done | bytes 2097168 | tf_op jit(solution)/shard_map/reduce_scatter | solution.py:10
  494.6 2.7 convert_element_type.3
Async XLA Ops:
  6.5 153.4 %all-gather.3.cloned.1.call-start = ((), (), s32[]{:S(2)}) async-start(), calls=%async_computation.1 | async-start | bytes 10485760 | tf_op jit(solution)/shard_map/all_gather | solution.py:8
  7.3 449.5 %all-gather.5.cloned.1.call-start = ((), (), s32[]{:S(2)}) async-start(), calls=%async_computation.2 | async-start | bytes 41943040 | tf_op jit(solution)/shard_map/all_gather | solution.py:9
  8.0 486.6 %reduce-scatter.2.cloned.1.call-start = ((), (), s32[]{:S(2)}) async-start(), calls=%async_computation.3 | async-start | bytes 6291456 | tf_op jit(solution)/shard_map/reduce_scatter | solution.py:10
Sparse Core Ops, SparseCore 0:
  8.9 150.9 all-gather.2
  161.8 294.9 all-gather.4
  481.6 12.9 reduce-scatter.1
where the time goes:
time: 505 us; the launch traced here: 504 us
  waiting for transfers between devices  463 us (92%)
  matrix products  24.8 us (5%)
  between operations  13.1 us (3%)
    all_gather x1, waiting for transfers between devices, local(): right_joined = lax.all_gather(right_matrix, 'row', axis=0, tiled=True)  297 us
    all_gather x1, waiting for transfers between devices, local(): left_rows = lax.all_gather(left_matrix, 'col', axis=1, tiled=True)  152 us
    dot_general x1, matrix products, local(): jnp.dot(left_rows, right_joined, preferred_element_type=jnp.float32)  24.8 us
    reduce_scatter x1, waiting for transfers between devices, local(): lax.psum_scatter(jnp.dot(left_rows, right_joined, preferred_element_type=...  13.1 us
  transfers between devices with their start and end apart: 3, of which 3 were waited for; matrix products, arithmetic and copies ran while one was open for 0% of the time, Pallas kernels for 0%

commit v1 on v0

v1 whole, which is shorter than its diff:
```python
import functools

import jax
import jax.numpy as jnp
from jax import lax
from jax.experimental import pallas as pl
from jax.experimental.pallas import tpu as pltpu
from jax.sharding import PartitionSpec as P

MESH = pl.DeviceIdType.MESH
CHUNKS = 4
TILE = 512


def kernel(R, NC, a_hbm, b_hbm, o_hbm, zbuf, pbuf, bbuf, cbuf, xbuf, rbuf, obuf,
           la, lb, zs, zr, ps, pr, ds, dr, cs, cr):
    l = lax.axis_index("layer")
    i = lax.axis_index("row")
    z = lax.axis_index("col")
    half = NC // 2
    N = bbuf.shape[1]
    tile = min(TILE, N)

    def a_copy(c):
        return pltpu.make_async_copy(a_hbm.at[c % 2, c // 2], zbuf.at[z, c], la.at[c])

    b_copy = pltpu.make_async_copy(b_hbm, bbuf, lb)

    def z_send(d, k, c):
        sign = 1 - 2 * d
        zb = z - sign * k
        return pltpu.make_async_remote_copy(
            src_ref=zbuf.at[zb, c], dst_ref=zbuf.at[zb, c],
            send_sem=zs.at[d, k, c], recv_sem=zr.at[d, k, c],
            device_id={"col": z + sign}, device_id_type=MESH)

    def z_recv(d, k, c):
        sign = 1 - 2 * d
        zb = z - sign * k
        return pltpu.make_async_remote_copy(
            src_ref=zbuf.at[zb, c], dst_ref=zbuf.at[zb, c],
            send_sem=zs.at[d, k - 1, c], recv_sem=zr.at[d, k - 1, c],
            device_id={"col": z - sign}, device_id_type=MESH)

    def p_send(zb, c):
        r = lax.rem(i - zb + R, R)
        return pltpu.make_async_remote_copy(
            src_ref=zbuf.at[zb, c], dst_ref=pbuf.at[r - 1, c],
            send_sem=ps.at[zb, c], recv_sem=pr.at[r - 1, c],
            device_id={"row": zb}, device_id_type=MESH)

    def p_recv(r, c):
        return pltpu.make_async_remote_copy(
            src_ref=pbuf.at[r - 1, c], dst_ref=pbuf.at[r - 1, c],
            send_sem=pr.at[r - 1, c], recv_sem=pr.at[r - 1, c],
            device_id={"row": lax.rem(i + r, R)}, device_id_type=MESH)

    def d_copy(r, c, q):
        return pltpu.make_async_remote_copy(
            src_ref=cbuf.at[r, c], dst_ref=xbuf.at[r, q],
            send_sem=ds.at[r, q], recv_sem=dr.at[r, q],
            device_id={"layer": 1 - l}, device_id_type=MESH)

    def c_copy(r, c, q):
        return pltpu.make_async_remote_copy(
            src_ref=cbuf.at[r, c], dst_ref=rbuf.at[R - r - 1, q],
            send_sem=cs.at[r - 1, q], recv_sem=cr.at[R - r - 1, q],
            device_id={"row": lax.rem(i + r, R)}, device_id_type=MESH)

    def c_recv(r, q):
        return pltpu.make_async_remote_copy(
            src_ref=rbuf.at[r - 1, q], dst_ref=rbuf.at[r - 1, q],
            send_sem=cr.at[r - 1, q], recv_sem=cr.at[r - 1, q],
            device_id={"row": lax.rem(i + r, R)}, device_id_type=MESH)

    for c in range(NC):
        a_copy(c).start()
    b_copy.start()

    barrier = pltpu.get_barrier_semaphore()
    for r in range(1, R):
        pl.semaphore_signal(barrier, inc=1, device_id={"row": lax.rem(i + r, R)}, device_id_type=MESH)
    pl.semaphore_signal(barrier, inc=1, device_id={"layer": 1 - l}, device_id_type=MESH)

    @pl.when(z > 0)
    def _():
        pl.semaphore_signal(barrier, inc=1, device_id={"col": z - 1}, device_id_type=MESH)

    @pl.when(z < R - 1)
    def _():
        pl.semaphore_signal(barrier, inc=1, device_id={"col": z + 1}, device_id_type=MESH)

    pl.semaphore_wait(barrier, R + (z > 0).astype(jnp.int32) + (z < R - 1).astype(jnp.int32))

    def outward(k, c, fn_z, fn_p):
        for d in range(2):
            sign = 1 - 2 * d
            zb = z - sign * k
            nxt = z + sign

            @pl.when((zb >= 0) & (zb < R) & (nxt >= 0) & (nxt < R))
            def _():
                fn_z(z_send(d, k, c))

    @pl.loop(0, NC)
    def _(c):
        a_copy(c).wait()
        outward(0, c, lambda x: x.start(), None)

        @pl.when(z != i)
        def _():
            p_send(z, c).start()

    b_copy.wait()

    def compute(c):
        h = lax.rem(c, 2)
        q = lax.div(c, 2)
        for r in range(R):
            if r > 0:
                p_recv(r, c).wait_recv()

            @pl.loop(0, N // tile)
            def _(n):
                cols = pl.ds(pl.multiple_of(n * tile, tile), tile)
                a = zbuf[i, c] if r == 0 else pbuf[r - 1, c]
                cbuf[r, c, :, cols] = jnp.dot(a, bbuf[:, cols], preferred_element_type=jnp.float32)

            @pl.when(h != l)
            def _():
                d_copy(r, c, q).start()

        @pl.when(h == l)
        def _():
            for r in (*range(1, R), 0):
                d_copy(r, c, q).wait_recv()

                @pl.loop(0, N // tile)
                def _(n):
                    cols = pl.ds(pl.multiple_of(n * tile, tile), tile)
                    cbuf[r, c, :, cols] = cbuf[r, c, :, cols] + xbuf[r, q, :, cols]

                if r > 0:
                    c_copy(r, c, q).start()

    far = jnp.abs(z - i)
    off = jnp.maximum(far - 1, 0) * NC

    @pl.loop(0, (R - 2) * NC + 2 * NC)
    def _(s):
        @pl.when(s < (R - 1) * NC)
        def _():
            k = lax.div(s, NC) + 1
            c = lax.rem(s, NC)
            for d in range(2):
                sign = 1 - 2 * d
                zb = z - sign * k
                nxt = z + sign

                @pl.when((zb >= 0) & (zb < R))
                def _():
                    z_recv(d, k, c).wait_recv()

                    @pl.when((nxt >= 0) & (nxt < R))
                    def _():
                        z_send(d, k, c).start()

                    @pl.when(zb != i)
                    def _():
                        p_send(zb, c).start()

        u = s - off

        @pl.when((u >= 0) & (u < 2 * NC) & (lax.rem(u + 2, 2) == 1))
        def _():
            compute(lax.div(u, 2))

    for q in range(half):
        c = 2 * q + l
        for r in range(1, R):
            c_recv(r, q).wait_recv()

        @pl.loop(0, N // tile)
        def _(n):
            cols = pl.ds(pl.multiple_of(n * tile, tile), tile)
            acc = cbuf[0, c, :, cols]
            for r in range(1, R):
                acc = acc + rbuf[r - 1, q, :, cols]
            obuf[q, :, cols] = acc.astype(jnp.bfloat16)

        pltpu.make_async_copy(obuf.at[q], o_hbm.at[q], la.at[q]).start()

    @pl.loop(0, NC)
    def _(c):
        for k in range(R):
            outward(k, c, lambda x: x.wait_send(), None)
        for zb in range(R):
            @pl.when(zb != i)
            def _():
                p_send(zb, c).wait_send()

    for q in range(half):
        for r in range(R):
            d_copy(r, 2 * q + 1 - l, q).wait_send()
            if r > 0:
                c_copy(r, 2 * q + l, q).wait_send()
        pltpu.make_async_copy(obuf.at[q], o_hbm.at[q], la.at[q]).wait()


def plain(left_matrix, right_matrix):
    left_rows = lax.all_gather(left_matrix, "col", axis=1, tiled=True)
    right_joined = lax.all_gather(right_matrix, "row", axis=0, tiled=True)
    summed = lax.psum_scatter(
        jnp.dot(left_rows, right_joined, preferred_element_type=jnp.float32),
        "layer",
        scatter_dimension=0,
        tiled=True,
    )
    return summed.astype(jnp.bfloat16)


def fused(R, left_matrix, right_matrix):
    rows, K = left_matrix.shape
    N = right_matrix.shape[1]
    NC = CHUNKS
    half = NC // 2
    CH = rows // NC
    dma = pltpu.SemaphoreType.DMA
    out = pl.pallas_call(
        functools.partial(kernel, R, NC),
        out_shape=jax.ShapeDtypeStruct((half, CH, N), jnp.bfloat16),
        in_specs=[pl.BlockSpec(memory_space=pl.ANY)] * 2,
        out_specs=pl.BlockSpec(memory_space=pl.ANY),
        scratch_shapes=[
            pltpu.VMEM((R, NC, CH, K), jnp.bfloat16),
            pltpu.VMEM((R - 1, NC, CH, K), jnp.bfloat16),
            pltpu.VMEM((K, N), jnp.bfloat16),
            pltpu.VMEM((R, NC, CH, N), jnp.float32),
            pltpu.VMEM((R, half, CH, N), jnp.float32),
            pltpu.VMEM((R - 1, half, CH, N), jnp.float32),
            pltpu.VMEM((half, CH, N), jnp.bfloat16),
            dma((NC,)), dma,
            dma((2, R, NC)), dma((2, R, NC)),
            dma((R, NC)), dma((R - 1, NC)),
            dma((R, half)), dma((R, half)),
            dma((R - 1, half)), dma((R - 1, half)),
        ],
        compiler_params=pltpu.CompilerParams(
            collective_id=0, has_side_effects=True, vmem_limit_bytes=67043328),
    )(left_matrix.reshape(2, half, CH, K), right_matrix)
    return out.reshape(half * CH, N)


def solution(mesh):
    shape = mesh.shape
    fits = shape["layer"] == 2 and shape["row"] == shape["col"]
    local = functools.partial(fused, shape["row"]) if fits else plain
    in_specs = (P("row", ("layer", "col")), P(("layer", "row"), "col"))
    out_specs = P(("row", "layer"), "col")
    return jax.shard_map(local, mesh=mesh, in_specs=in_specs, out_specs=out_specs, check_vma=False)
```

time: 505 us -> 355 us (0.70)
  waiting for transfers between devices: 463 us -> 0 us
  Pallas kernels: 0 us -> 352 us
  matrix products: 24.8 us -> 0 us
  between operations: 13.1 us -> 0.01 us
    all_gather x2 -> x0, waiting for transfers between devices: 449 us -> none  [the longest x1 297 us: local(): right_joined = lax.all_gather(right_matrix, 'row', axis=0, tiled=True)]
    pallas_call x0 -> x1, Pallas kernels: none -> 352 us  [fused(): pl.pallas_call(functools.partial(kernel, R, NC), out_shape=jax.ShapeDtype...]
    dot_general x1 -> x0, matrix products: 24.8 us -> none  [local(): jnp.dot(left_rows, right_joined, preferred_element_type=jnp.float32)]
    reduce_scatter x1 -> x0, waiting for transfers between devices: 13.1 us -> none  [local(): lax.psum_scatter(jnp.dot(left_rows, right_joined, preferred_element_type=...]
  transfers between devices with their start and end apart: 3 -> 0, of which waited for: 3 -> 0; matrix products, arithmetic and copies ran while one was open for 0% -> 0% of each run, Pallas kernels for 0% -> 0%
where the time goes in v1:
time: 355 us; the launch traced here: 354 us
  Pallas kernels  352 us (99%)
    pallas_call x1, Pallas kernels, fused(): pl.pallas_call(functools.partial(kernel, R, NC), out_shape=jax.ShapeDtype...  352 us

profile of v1, /device:TPU:5, one launch (start us, length us, event | category | flops | bytes accessed | tf_op | source)
XLA Modules:
  0.0 354.4 jit_solution(10550163901688587275)
XLA Ops:
  0.0 352.1 %shard_map.28 = bf16[2,128,2048]{2,1,0:T(8,128)(2,1)} custom-call(bf16[2,2,128,2048]{3,2,1,0:T(8,128)(2,1)} %bitcast.3, bf16[2048,2048]{1,0:T(8,128)(2,1)} %b_hbm.1), custom_call_target="tpu_custom_call" | custom-call | tf_op jit(solution)/shard_map/pallas_call | solution.py:229
  352.1 2.3 copy.4

commit v2 on v0

v2 whole, which is shorter than its diff:
```python
import functools

import jax
import jax.numpy as jnp
from jax import lax
from jax.experimental import pallas as pl
from jax.experimental.pallas import tpu as pltpu
from jax.sharding import PartitionSpec as P

MESH = pl.DeviceIdType.MESH
CHUNKS = 8
STRIPS = 8


def kernel(R, NC, NB, a_hbm, b_hbm, o_hbm, zbuf, pbuf, bown, bin_, cbuf, xbuf, rbuf, obuf,
           la, lb, zs, zr, ps, pr, bs, br, ds, dr, cs, cr, lo):
    l = lax.axis_index("layer")
    i = lax.axis_index("row")
    z = lax.axis_index("col")
    x = lax.rem(i, 2)
    y = lax.div(i, 2)
    xn = 2 * y + 1 - x
    yn = 2 * (1 - y) + x
    rows = zbuf.shape[1]
    CH = rows // NC
    half = rows // 2
    W = bown.shape[2]

    def chunk(c):
        return pl.ds(pl.multiple_of(c * CH, CH), CH)

    def a_copy(c):
        return pltpu.make_async_copy(a_hbm.at[chunk(c)], zbuf.at[z, chunk(c)], la.at[c])

    def b_copy(n):
        return pltpu.make_async_copy(b_hbm.at[:, pl.ds(n * W, W)], bown.at[n], lb.at[n])

    def remote(src, dst, send, recv, **where):
        return pltpu.make_async_remote_copy(
            src_ref=src, dst_ref=dst, send_sem=send, recv_sem=recv,
            device_id=where, device_id_type=MESH)

    def z_send(d, k, c):
        sign = 1 - 2 * d
        zb = z - sign * k
        return remote(zbuf.at[zb, chunk(c)], zbuf.at[zb, chunk(c)], zs.at[d, k, c], zr.at[d, k, c], col=z + sign)

    def z_recv(d, k, c):
        sign = 1 - 2 * d
        zb = z - sign * k
        return remote(zbuf.at[zb, chunk(c)], zbuf.at[zb, chunk(c)], zs.at[d, k - 1, c], zr.at[d, k - 1, c], col=z - sign)

    def p_send(zb, c):
        v = lax.div(zb, 2)
        return remote(zbuf.at[zb, chunk(c)], pbuf.at[v, chunk(c)], ps.at[v, c], pr.at[v, c], row=xn)

    def b_send(n):
        return remote(bown.at[n], bin_.at[n], bs.at[n], br.at[n], row=yn)

    def d_send(n):
        return remote(cbuf.at[n, 1 - l], xbuf.at[n], ds.at[n], dr.at[n], layer=1 - l)

    def c_send(n):
        return remote(cbuf.at[n, l, 1], rbuf.at[n], cs.at[n], cr.at[n], row=xn)

    for c in range(NC):
        a_copy(c).start()
    for n in range(NB):
        b_copy(n).start()

    barrier = pltpu.get_barrier_semaphore()
    pl.semaphore_signal(barrier, inc=1, device_id={"row": xn}, device_id_type=MESH)
    pl.semaphore_signal(barrier, inc=1, device_id={"row": yn}, device_id_type=MESH)
    pl.semaphore_signal(barrier, inc=1, device_id={"layer": 1 - l}, device_id_type=MESH)

    @pl.when(z > 0)
    def _():
        pl.semaphore_signal(barrier, inc=1, device_id={"col": z - 1}, device_id_type=MESH)

    @pl.when(z < R - 1)
    def _():
        pl.semaphore_signal(barrier, inc=1, device_id={"col": z + 1}, device_id_type=MESH)

    pl.semaphore_wait(barrier, 3 + (z > 0).astype(jnp.int32) + (z < R - 1).astype(jnp.int32))

    def outward(k, c, act):
        for d in range(2):
            sign = 1 - 2 * d
            zb = z - sign * k
            nxt = z + sign

            @pl.when((zb >= 0) & (zb < R) & (nxt >= 0) & (nxt < R))
            def _():
                act(z_send(d, k, c))

    @pl.loop(0, NC)
    def _(c):
        a_copy(c).wait()
        outward(0, c, lambda s: s.start())

        @pl.when(lax.rem(z, 2) != x)
        def _():
            p_send(z, c).start()

    @pl.loop(0, NB)
    def _(n):
        b_copy(n).wait()
        b_send(n).start()

    @pl.loop(0, (R - 1) * NC)
    def _(s):
        k = lax.div(s, NC) + 1
        c = lax.rem(s, NC)
        for d in range(2):
            sign = 1 - 2 * d
            zb = z - sign * k
            nxt = z + sign

            @pl.when((zb >= 0) & (zb < R))
            def _():
                z_recv(d, k, c).wait_recv()

                @pl.when((nxt >= 0) & (nxt < R))
                def _():
                    z_send(d, k, c).start()

                @pl.when(lax.rem(zb + R, 2) != x)
                def _():
                    p_send(zb, c).start()

    @pl.loop(0, NC)
    def _(c):
        for v in range(R // 2):
            remote(pbuf.at[v, chunk(c)], pbuf.at[v, chunk(c)], pr.at[v, c], pr.at[v, c], row=xn).wait_recv()

    def settle(n):
        d_send(n).wait_recv()
        cbuf[n, l, 1] = cbuf[n, l, 1] + xbuf[n, 1]
        c_send(n).start()
        cbuf[n, l, 0] = cbuf[n, l, 0] + xbuf[n, 0]

    def finish(n):
        c_send(n).wait_recv()
        obuf[n] = (cbuf[n, l, 0] + rbuf[n]).astype(jnp.bfloat16)
        pltpu.make_async_copy(obuf.at[n], o_hbm.at[:, pl.ds(n * W, W)], lo.at[n]).start()

    @pl.loop(0, NB + 1)
    def _(n):
        @pl.when(n < NB)
        def _():
            b_send(n).wait_recv()
            for s, left in ((1, pbuf), (0, zbuf)):
                near, far = (y, 1 - y) if s else (2 * y + x, 2 * (1 - y) + x)
                for h in range(2):
                    part = pl.ds(h * half, half)
                    cbuf[n, h, s] = (
                        jnp.dot(left[near, part], bown[n], preferred_element_type=jnp.float32)
                        + jnp.dot(left[far, part], bin_[n], preferred_element_type=jnp.float32))
            d_send(n).start()

        @pl.when(n > 0)
        def _():
            settle(n - 1)

    @pl.loop(0, NB)
    def _(n):
        finish(n)

    @pl.loop(0, NC)
    def _(c):
        for k in range(R):
            outward(k, c, lambda s: s.wait_send())
        for v in range(R // 2):
            p_send(2 * v + 1 - x, c).wait_send()

    @pl.loop(0, NB)
    def _(n):
        b_send(n).wait_send()
        d_send(n).wait_send()
        c_send(n).wait_send()
        pltpu.make_async_copy(obuf.at[n], o_hbm.at[:, pl.ds(n * W, W)], lo.at[n]).wait()


def plain(left_matrix, right_matrix):
    left_rows = lax.all_gather(left_matrix, "col", axis=1, tiled=True)
    right_joined = lax.all_gather(right_matrix, "row", axis=0, tiled=True)
    summed = lax.psum_scatter(
        jnp.dot(left_rows, right_joined, preferred_element_type=jnp.float32),
        "layer",
        scatter_dimension=0,
        tiled=True,
    )
    return summed.astype(jnp.bfloat16)


def fused(R, left_matrix, right_matrix):
    rows, K = left_matrix.shape
    N = right_matrix.shape[1]
    NC, NB = CHUNKS, STRIPS
    W, half = N // NB, rows // 2
    bf16, f32 = jnp.bfloat16, jnp.float32
    dma = pltpu.SemaphoreType.DMA
    return pl.pallas_call(
        functools.partial(kernel, R, NC, NB),
        out_shape=jax.ShapeDtypeStruct((half, N), bf16),
        in_specs=[pl.BlockSpec(memory_space=pl.ANY)] * 2,
        out_specs=pl.BlockSpec(memory_space=pl.ANY),
        scratch_shapes=[
            pltpu.VMEM((R, rows, K), bf16),
            pltpu.VMEM((R // 2, rows, K), bf16),
            pltpu.VMEM((NB, K, W), bf16),
            pltpu.VMEM((NB, K, W), bf16),
            pltpu.VMEM((NB, 2, 2, half, W), f32),
            pltpu.VMEM((NB, 2, half, W), f32),
            pltpu.VMEM((NB, half, W), f32),
            pltpu.VMEM((NB, half, W), bf16),
            dma((NC,)), dma((NB,)),
            dma((2, R, NC)), dma((2, R, NC)),
            dma((R // 2, NC)), dma((R // 2, NC)),
            dma((NB,)), dma((NB,)),
            dma((NB,)), dma((NB,)),
            dma((NB,)), dma((NB,)),
            dma((NB,)),
        ],
        compiler_params=pltpu.CompilerParams(
            collective_id=0, has_side_effects=True, vmem_limit_bytes=67043328),
    )(left_matrix, right_matrix)


def solution(mesh):
    shape = mesh.shape
    fits = shape["layer"] == 2 and shape["row"] == shape["col"] == 4
    local = functools.partial(fused, shape["row"]) if fits else plain
    in_specs = (P("row", ("layer", "col")), P(("layer", "row"), "col"))
    out_specs = P(("row", "layer"), "col")
    return jax.shard_map(local, mesh=mesh, in_specs=in_specs, out_specs=out_specs, check_vma=False)
```

time: 505 us -> 208 us (0.41)
  waiting for transfers between devices: 463 us -> 0 us
  Pallas kernels: 0 us -> 202 us
  matrix products: 24.8 us -> 0 us
  between operations: 13.1 us -> 0.01 us
    all_gather x2 -> x0, waiting for transfers between devices: 449 us -> none  [the longest x1 297 us: local(): right_joined = lax.all_gather(right_matrix, 'row', axis=0, tiled=True)]
    pallas_call x0 -> x1, Pallas kernels: none -> 202 us  [fused(): pl.pallas_call(functools.partial(kernel, R, NC, NB), out_shape=jax.ShapeD...]
    dot_general x1 -> x0, matrix products: 24.8 us -> none  [local(): jnp.dot(left_rows, right_joined, preferred_element_type=jnp.float32)]
    reduce_scatter x1 -> x0, waiting for transfers between devices: 13.1 us -> none  [local(): lax.psum_scatter(jnp.dot(left_rows, right_joined, preferred_element_type=...]
  transfers between devices with their start and end apart: 3 -> 0, of which waited for: 3 -> 0; matrix products, arithmetic and copies ran while one was open for 0% -> 0% of each run, Pallas kernels for 0% -> 0%
where the time goes in v2:
time: 208 us; the launch traced here: 204 us
  Pallas kernels  202 us (97%)
  local copies, waits for them, and re-layouts  2.3 us (1%)
    pallas_call x1, Pallas kernels, fused(): pl.pallas_call(functools.partial(kernel, R, NC, NB), out_shape=jax.ShapeD...  202 us

profile of v2, /device:TPU:5, one launch (start us, length us, event | category | flops | bytes accessed | tf_op | source)
XLA Modules:
  0.0 203.8 jit_solution(9232833914851515402)
XLA Ops:
  0.0 201.5 %shard_map.28 = bf16[256,2048]{1,0:T(8,128)(2,1)} custom-call(bf16[512,2048]{1,0:T(8,128)(2,1)} %a_hbm.1, bf16[2048,2048]{1,0:T(8,128)(2,1)} %b_hbm.1), custom_call_target="tpu_custom_call" | custom-call | tf_op jit(solution)/shard_map/pallas_call | solution.py:203
  201.5 2.3 %copy.4 = bf16[256,2048]{1,0:T(8,128)(2,1)} copy(bf16[256,2048]{1,0:T(8,128)(2,1)} %shard_map.28) | data formatting | bytes 2097152

commit v3 on v2

--- a/solution.py
+++ b/solution.py
@@ -10,6 +10,7 @@
 MESH = pl.DeviceIdType.MESH
 CHUNKS = 8
 STRIPS = 8
+EARLY = 5
 
 
 def kernel(R, NC, NB, a_hbm, b_hbm, o_hbm, zbuf, pbuf, bown, bin_, cbuf, xbuf, rbuf, obuf,
@@ -107,8 +108,7 @@
         b_copy(n).wait()
         b_send(n).start()
 
-    @pl.loop(0, (R - 1) * NC)
-    def _(s):
+    def z_step(s):
         k = lax.div(s, NC) + 1
         c = lax.rem(s, NC)
         for d in range(2):
@@ -128,10 +128,21 @@
                 def _():
                     p_send(zb, c).start()
 
-    @pl.loop(0, NC)
-    def _(c):
+    def p_wait(c):
         for v in range(R // 2):
             remote(pbuf.at[v, chunk(c)], pbuf.at[v, chunk(c)], pr.at[v, c], pr.at[v, c], row=xn).wait_recv()
+
+    def multiply(n, h):
+        part = pl.ds(h * half, half)
+        for s, left in ((1, pbuf), (0, zbuf)):
+            near, far = (y, 1 - y) if s else (2 * y + x, 2 * (1 - y) + x)
+            cbuf[n, h, s] = (
+                jnp.dot(left[near, part], bown[n], preferred_element_type=jnp.float32)
+                + jnp.dot(left[far, part], bin_[n], preferred_element_type=jnp.float32))
+
+        @pl.when(h != l)
+        def _():
+            d_send(n).start()
 
     def settle(n):
         d_send(n).wait_recv()
@@ -144,25 +155,55 @@
         obuf[n] = (cbuf[n, l, 0] + rbuf[n]).astype(jnp.bfloat16)
         pltpu.make_async_copy(obuf.at[n], o_hbm.at[:, pl.ds(n * W, W)], lo.at[n]).start()
 
-    @pl.loop(0, NB + 1)
-    def _(n):
-        @pl.when(n < NB)
+    def sweep(h, first):
+        @pl.loop(0, EARLY + 1)
+        def _(n):
+            @pl.when(n < EARLY)
+            def _():
+                if first:
+                    b_send(n).wait_recv()
+                multiply(n, h)
+
+            @pl.when((n > 0) & (l == h))
+            def _():
+                settle(n - 1)
+
+    pause = (R - 2) * NC + NC // 2 + 2
+
+    @pl.loop(0, pause)
+    def _(s):
+        z_step(s)
+
+    @pl.loop(0, NC // 2)
+    def _(c):
+        p_wait(c)
+
+    sweep(0, True)
+
+    @pl.loop(pause, (R - 1) * NC)
+    def _(s):
+        z_step(s)
+
+    @pl.loop(NC // 2, NC)
+    def _(c):
+        p_wait(c)
+
+    sweep(1, False)
+
+    @pl.loop(EARLY, NB)
+    def _(n):
+        @pl.when(n == NB - 1)
         def _():
-            b_send(n).wait_recv()
-            for s, left in ((1, pbuf), (0, zbuf)):
-                near, far = (y, 1 - y) if s else (2 * y + x, 2 * (1 - y) + x)
-                for h in range(2):
-                    part = pl.ds(h * half, half)
-                    cbuf[n, h, s] = (
-                        jnp.dot(left[near, part], bown[n], preferred_element_type=jnp.float32)
-                        + jnp.dot(left[far, part], bin_[n], preferred_element_type=jnp.float32))
-            d_send(n).start()
-
-        @pl.when(n > 0)
-        def _():
-            settle(n - 1)
-
-    @pl.loop(0, NB)
+            @pl.loop(0, NB - 2)
+            def _(m):
+                finish(m)
+
+        b_send(n).wait_recv()
+        multiply(n, 0)
+        multiply(n, 1)
+        settle(n)
+
+    @pl.loop(NB - 2, NB)
     def _(n):
         finish(n)
 

time: 208 us -> 218 us (1.048)
  Pallas kernels: 202 us -> 213 us
    pallas_call x1, Pallas kernels: 202 us -> 213 us  [fused(): pl.pallas_call(functools.partial(kernel, R, NC, NB), out_shape=jax.ShapeD...]
where the time goes in v3:
time: 218 us; the launch traced here: 215 us
  Pallas kernels  213 us (98%)
  local copies, waits for them, and re-layouts  2.3 us (1%)
    pallas_call x1, Pallas kernels, fused(): pl.pallas_call(functools.partial(kernel, R, NC, NB), out_shape=jax.ShapeD...  213 us

profile of v3, /device:TPU:5, one launch (start us, length us, event | category | flops | bytes accessed | tf_op | source)
XLA Modules:
  0.0 215.1 jit_solution(13006338953326990943)
XLA Ops:
  0.0 212.8 %shard_map.28 = bf16[256,2048]{1,0:T(8,128)(2,1)} custom-call(bf16[512,2048]{1,0:T(8,128)(2,1)} %a_hbm.1, bf16[2048,2048]{1,0:T(8,128)(2,1)} %b_hbm.1), custom_call_target="tpu_custom_call" | custom-call | tf_op jit(solution)/shard_map/pallas_call | solution.py:244
  212.8 2.3 %copy.4 = bf16[256,2048]{1,0:T(8,128)(2,1)} copy(bf16[256,2048]{1,0:T(8,128)(2,1)} %shard_map.28) | data formatting | bytes 2097152

commit v4 on v2

--- a/solution.py
+++ b/solution.py
@@ -10,6 +10,7 @@
 MESH = pl.DeviceIdType.MESH
 CHUNKS = 8
 STRIPS = 8
+LATE = 5
 
 
 def kernel(R, NC, NB, a_hbm, b_hbm, o_hbm, zbuf, pbuf, bown, bin_, cbuf, xbuf, rbuf, obuf,
@@ -144,23 +145,28 @@
         obuf[n] = (cbuf[n, l, 0] + rbuf[n]).astype(jnp.bfloat16)
         pltpu.make_async_copy(obuf.at[n], o_hbm.at[:, pl.ds(n * W, W)], lo.at[n]).start()
 
-    @pl.loop(0, NB + 1)
-    def _(n):
-        @pl.when(n < NB)
-        def _():
-            b_send(n).wait_recv()
-            for s, left in ((1, pbuf), (0, zbuf)):
-                near, far = (y, 1 - y) if s else (2 * y + x, 2 * (1 - y) + x)
-                for h in range(2):
-                    part = pl.ds(h * half, half)
-                    cbuf[n, h, s] = (
-                        jnp.dot(left[near, part], bown[n], preferred_element_type=jnp.float32)
-                        + jnp.dot(left[far, part], bin_[n], preferred_element_type=jnp.float32))
-            d_send(n).start()
-
-        @pl.when(n > 0)
+    def multiply(n):
+        b_send(n).wait_recv()
+        for s, left in ((1, pbuf), (0, zbuf)):
+            near, far = (y, 1 - y) if s else (2 * y + x, 2 * (1 - y) + x)
+            for h in range(2):
+                part = pl.ds(h * half, half)
+                cbuf[n, h, s] = (
+                    jnp.dot(left[near, part], bown[n], preferred_element_type=jnp.float32)
+                    + jnp.dot(left[far, part], bin_[n], preferred_element_type=jnp.float32))
+        d_send(n).start()
+
+    @pl.loop(0, NB)
+    def _(n):
+        multiply(n)
+
+        @pl.when((n > 0) & (n <= LATE))
         def _():
             settle(n - 1)
+
+        @pl.when(n >= LATE)
+        def _():
+            settle(n)
 
     @pl.loop(0, NB)
     def _(n):

time: 208 us -> 204 us (0.981)
  Pallas kernels: 202 us -> 199 us
    pallas_call x1, Pallas kernels: 202 us -> 199 us  [fused(): pl.pallas_call(functools.partial(kernel, R, NC, NB), out_shape=jax.ShapeD...]
where the time goes in v4:
time: 204 us; the launch traced here: 201 us
  Pallas kernels  199 us (98%)
  local copies, waits for them, and re-layouts  2.3 us (1%)
    pallas_call x1, Pallas kernels, fused(): pl.pallas_call(functools.partial(kernel, R, NC, NB), out_shape=jax.ShapeD...  199 us

profile of v4, /device:TPU:5, one launch (start us, length us, event | category | flops | bytes accessed | tf_op | source)
XLA Modules:
  0.0 201.4 jit_solution(9895446177209558766)
XLA Ops:
  0.0 199.1 %shard_map.28 = bf16[256,2048]{1,0:T(8,128)(2,1)} custom-call(bf16[512,2048]{1,0:T(8,128)(2,1)} %a_hbm.1, bf16[2048,2048]{1,0:T(8,128)(2,1)} %b_hbm.1), custom_call_target="tpu_custom_call" | custom-call | tf_op jit(solution)/shard_map/pallas_call | solution.py:209
  199.1 2.3 %copy.4 = bf16[256,2048]{1,0:T(8,128)(2,1)} copy(bf16[256,2048]{1,0:T(8,128)(2,1)} %shard_map.28) | data formatting | bytes 2097152
